TPU v7x, 32 devices: a whole 2x2x4 slice. The times are simulated.
32 devices in a mesh: dp: 4 (over y, core), seq: 8 (over z, x).
Axes of the slice: x: 2, y: 2, z: 4, core: 2. Of those that a mesh axis runs over, the one named last changes fastest.
Arguments:
- queries: bfloat16 [32, 2048, 512], P('dp', 'seq'), may hold values from -6 to 6
- enc_keys: bfloat16 [32, 2048, 512], P('dp', 'seq'), may hold values from -6 to 6
- enc_values: bfloat16 [32, 2048, 512], P('dp', 'seq'), may hold values from -6 to 6
- dec_ids: int32 [32, 2048], P('dp', 'seq'), may hold values from 0 to 15, never falling along the last dimension, each value on 1 to 512 neighbouring positions
- enc_ids: int32 [32, 2048], P('dp', 'seq'), may hold values from 0 to 15, never falling along the last dimension, each value on 1 to 512 neighbouring positions
Outputs:
- context: bfloat16 [32, 2048, 512], P('dp', 'seq')
Inputs may be any that keep to these rules, and one draw needn't show every extreme that they name: `dec_ids`: along each row the numbers never fall; every number from 0 to 15 occurs in every row; a document holds 1 to 512 positions of a row, and some document holds exactly 512. `enc_ids`: along each row the numbers never fall; every number from 0 to 15 occurs in every row; a document holds 1 to 512 positions of a row, and some document holds exactly 512.
All inputs are finite; a program needn't handle non-finite values.
Results may differ from a plain program's by a relative error of at most 0.0047.
Values may be sent and summed in bfloat16 or wider, within the bound.
No kernel may reach another device: no remote copies, remote signals or barrier semaphores. Data moves between devices by JAX's collectives and lax.ppermute only.
A program may use at most 128 MiB of HBM per device.

v0:
```python
import jax
import jax.numpy as jnp
from jax import lax
from jax.sharding import PartitionSpec as P

HEAD_DIM = 64


masked_score = -1e30


def shortened(value):

    def short(part):
        return part.astype(jnp.bfloat16) if part.dtype == jnp.float32 else part

    return jax.tree.map(short, value)


def attend_dense(query_row, key_row, value_row, dec_row, enc_row, head_count):
    length = query_row.shape[0]
    query_heads = query_row.reshape(length, head_count, HEAD_DIM)
    key_heads = key_row.reshape(length, head_count, HEAD_DIM)
    value_heads = value_row.reshape(length, head_count, HEAD_DIM)
    query_span = min(512, length)
    pieces = []
    for offset in range(0, length, query_span):
        scores = jnp.einsum(
            "qhd,khd->hqk",
            query_heads[offset : offset + query_span],
            key_heads,
            preferred_element_type=jnp.float32,
        )
        allowed = (dec_row[offset : offset + query_span][:, None] == enc_row[None, :])[None]
        scores = jnp.where(allowed, scores, masked_score)
        row_peak = jnp.max(scores, axis=2, keepdims=True)
        expos = jnp.where(allowed, jnp.exp(scores - row_peak), 0.0)
        row_total = jnp.sum(expos, axis=2, keepdims=True)
        weights = (expos / row_total).astype(jnp.bfloat16)
        summed = jnp.einsum(
            "hqk,khd->qhd", weights, value_heads, preferred_element_type=jnp.float32
        )
        pieces.append(summed.reshape(query_span, head_count * HEAD_DIM).astype(jnp.bfloat16))
    return jnp.concatenate(pieces, axis=0)


def local(queries, enc_keys, enc_values, dec_ids, enc_ids):
    group = lax.axis_size("seq")
    dec_spread = jnp.broadcast_to(
        dec_ids.astype(jnp.bfloat16)[:, :, None], (dec_ids.shape[0], dec_ids.shape[1], group)
    )
    enc_spread = jnp.broadcast_to(
        enc_ids.astype(jnp.bfloat16)[:, :, None], (enc_ids.shape[0], enc_ids.shape[1], group)
    )
    members = (
        lax.all_to_all(queries, "seq", split_axis=2, concat_axis=1, tiled=True),
        lax.all_to_all(enc_keys, "seq", split_axis=2, concat_axis=1, tiled=True),
        lax.all_to_all(enc_values, "seq", split_axis=2, concat_axis=1, tiled=True),
        lax.all_to_all(dec_spread, "seq", split_axis=2, concat_axis=1, tiled=True),
        lax.all_to_all(enc_spread, "seq", split_axis=2, concat_axis=1, tiled=True),
    )
    dec_rows = members[3][:, :, 0].astype(jnp.int32)
    enc_rows = members[4][:, :, 0].astype(jnp.int32)
    query_rows = members[0]
    key_rows = members[1]
    value_rows = members[2]
    head_count = query_rows.shape[2] // HEAD_DIM

    def one_row(members):
        return attend_dense(members[0], members[1], members[2], members[3], members[4], head_count)

    attended = lax.map(one_row, (query_rows, key_rows, value_rows, dec_rows, enc_rows))
    return lax.all_to_all(
        shortened(attended), "seq", split_axis=1, concat_axis=2, tiled=True
    ).astype(attended.dtype)


def solution(mesh):
    in_specs = (
        P("dp", "seq", None),
        P("dp", "seq", None),
        P("dp", "seq", None),
        P("dp", "seq"),
        P("dp", "seq"),
    )
    out_specs = P("dp", "seq", None)
    return jax.shard_map(local, mesh=mesh, in_specs=in_specs, out_specs=out_specs, check_vma=False)
```

profile of v0, /device:TPU:0, one launch (start us, length us, event | category | flops | bytes accessed | tf_op | source)
XLA Modules:
  0.0 412.9 jit_solution(16733577638339409978)
XLA Ops:
  1.3 7.3 %all-to-all-start.1 = ((bf16[8,256,8]{1,0,2:T(8,128)(2,1)}), bf16[8,256,8]{1,0,2:T(8,128)(2,1)S(1)}, u32[]{:S(2)}, u32[]{:S(2)}) async-start(bf16[8,256,8]{1,0,2:T(8,128)(2,1)} %broadcast_in_dim.23), calls=%async_computation.1 | async-start | bytes 65536 | tf_op jit(solution)/shard_map/all_to_all | solution.py:59
  9.3 6.0 %all-to-all-done.1 = bf16[8,256,8]{1,0,2:T(8,128)(2,1)S(1)} async-done(((bf16[8,256,8]{1,0,2:T(8,128)(2,1)}), bf16[8,256,8]{1,0,2:T(8,128)(2,1)S(1)}, u32[]{:S(2)}, u32[]{:S(2)}) %all-to-all-start.1) | async-done | bytes 32800 | tf_op jit(solution)/shard_map/all_to_all | solution.py:59
  15.9 3.3 all-to-all-start.2
  19.2 4.5 %copy.25 = bf16[8,256,512]{1,0,2:T(8,128)(2,1)} copy(bf16[8,256,512]{2,1,0:T(8,128)(2,1)} %param.9) | data formatting | bytes 4194304 | tf_op args[2]
  23.7 2.1 all-to-all-done.2
  25.9 3.8 all-to-all-start
  29.7 4.5 %copy.28 = bf16[8,256,512]{1,0,2:T(8,128)(2,1)} copy(bf16[8,256,512]{2,1,0:T(8,128)(2,1)} %param.7) | data formatting | bytes 4194304 | tf_op args[0]
  34.2 42.1 %all-to-all-done = bf16[8,256,512]{1,0,2:T(8,128)(2,1)S(1)} async-done(((bf16[8,256,512]{1,0,2:T(8,128)(2,1)}), bf16[8,256,512]{1,0,2:T(8,128)(2,1)S(1)}, u32[]{:S(2)}, u32[]{:S(2)}) %all-to-all-start) | async-done | bytes 2097184 | tf_op jit(solution)/shard_map/all_to_all | solution.py:58
  76.3 4.4 %all-to-all-start.3 = ((bf16[8,256,512]{1,0,2:T(8,128)(2,1)}), bf16[8,256,512]{1,0,2:T(8,128)(2,1)}, u32[]{:S(2)}, u32[]{:S(2)}) async-start(bf16[8,256,512]{1,0,2:T(8,128)(2,1)} %copy.28), calls=%async_computation.3 | async-start | bytes 4194304 | tf_op jit(solution)/shard_map/all_to_all | solution.py:56
  80.7 4.5 %copy.31 = bf16[8,256,512]{1,0,2:T(8,128)(2,1)} copy(bf16[8,256,512]{2,1,0:T(8,128)(2,1)} %param.8) | data formatting | bytes 4194304 | tf_op args[1]
  85.2 43.1 %all-to-all-done.3 = bf16[8,256,512]{1,0,2:T(8,128)(2,1)} async-done(((bf16[8,256,512]{1,0,2:T(8,128)(2,1)}), bf16[8,256,512]{1,0,2:T(8,128)(2,1)}, u32[]{:S(2)}, u32[]{:S(2)}) %all-to-all-start.3) | async-done | bytes 2097184 | tf_op jit(solution)/shard_map/all_to_all | solution.py:56
  128.3 4.4 %all-to-all-start.4 = ((bf16[8,256,512]{1,0,2:T(8,128)(2,1)}), bf16[8,256,512]{1,0,2:T(8,128)(2,1)}, u32[]{:S(2)}, u32[]{:S(2)}) async-start(bf16[8,256,512]{1,0,2:T(8,128)(2,1)} %copy.31), calls=%async_computation.4 | async-start | bytes 4194304 | tf_op jit(solution)/shard_map/all_to_all | solution.py:57
  132.7 3.5 copy.42
  136.3 5.0 %copy.44 = bf16[8,8,256,64]{3,2,1,0:T(8,128)(2,1)} copy(bf16[8,8,256,64]{2,0,3,1:T(8,128)(2,1)} %bitcast.36) | data formatting | bytes 4194304 | tf_op jit(solution)/shard_map/while | solution.py:72
  141.3 39.2 %all-to-all-done.4 = bf16[8,256,512]{1,0,2:T(8,128)(2,1)} async-done(((bf16[8,256,512]{1,0,2:T(8,128)(2,1)}), bf16[8,256,512]{1,0,2:T(8,128)(2,1)}, u32[]{:S(2)}, u32[]{:S(2)}) %all-to-all-start.4) | async-done | bytes 2097184 | tf_op jit(solution)/shard_map/all_to_all | solution.py:57
  180.5 5.0 %copy.46 = bf16[8,8,256,64]{3,2,1,0:T(8,128)(2,1)} copy(bf16[8,8,256,64]{2,0,3,1:T(8,128)(2,1)} %bitcast.40) | data formatting | bytes 4194304 | tf_op jit(solution)/shard_map/while | solution.py:72
  185.5 150.7 %while.10 = (s32[]{:T(128)}, bf16[8,2048,64]{1,2,0:T(8,128)(2,1)S(1)}, bf16[8,2048,64]{2,1,0:T(8,128)(2,1)}, s32[8,2048]{1,0:T(8,128)S(1)}, s32[8,2048]{1,0:T(8,...) while((s32[]{:T(128)}, ...), condition=%wide.region_9.10_spmd, body=%wide.region_0.9_spmd.sunk | while | flops 1133637632 | bytes 72773864 | solution.py:72
  185.6 2.0 fusion.83
  187.5 1.8 fusion.81
  189.4 1.8 fusion.84
  191.2 3.9 fusion.85
  196.5 3.4 fusion.86
  202.8 1.4 fusion.87
  204.4 2.0 fusion.83
  206.4 1.8 fusion.81
  208.2 1.8 fusion.84
  210.1 3.9 fusion.85
  215.4 3.4 fusion.86
  223.3 2.0 fusion.83
  225.2 1.8 fusion.81
  227.0 1.8 fusion.84
  228.9 3.9 fusion.85
  234.2 3.4 fusion.86
  242.1 2.0 fusion.83
  244.0 1.8 fusion.81
  245.9 1.8 fusion.84
  247.7 3.9 fusion.85
  253.0 3.4 fusion.86
  260.9 2.0 fusion.83
  262.9 1.8 fusion.81
  264.7 1.8 fusion.84
  266.6 3.9 fusion.85
  271.9 3.4 fusion.86
  279.8 2.0 fusion.83
  281.7 1.8 fusion.81
  283.6 1.8 fusion.84
  285.4 3.9 fusion.85
  290.7 3.4 fusion.86
  298.6 2.0 fusion.83
  300.6 1.8 fusion.81
  302.4 1.8 fusion.84
  304.2 3.9 fusion.85
  309.6 3.4 fusion.86
  317.4 2.0 fusion.83
  319.4 1.8 fusion.81
  321.2 1.8 fusion.84
  323.1 3.9 fusion.85
  328.4 3.4 fusion.86
  336.2 4.3 %copy.37 = bf16[8,2048,64]{2,0,1:T(8,128)(2,1)} copy(bf16[8,2048,64]{1,2,0:T(8,128)(2,1)S(1)} %get-tuple-element.42) | data formatting | bytes 4194304 | tf_op jit(solution)/shard_map/while | solution.py:72
  340.5 6.4 %reshape.166 = bf16[8,2,65536]{2,1,0:T(2,128)(2,1)S(1)} reshape(bf16[2048,8,64]{2,1,0:T(8,128)(2,1)} %bitcast.147) | data formatting | bytes 4194304
  346.8 51.8 %all_to_all.90 = bf16[8,2,65536]{2,1,0:T(2,128)(2,1)} all-to-all(bf16[8,2,65536]{2,1,0:T(2,128)(2,1)S(1)} %reshape.166), channel_id=1, replica_groups=mesh['dp'=4,'seq'=8] {'seq'}, dimensions={0} | all-to-all | bytes 4194304 | tf_op jit(solution)/shard_map/all_to_all | solution.py:73
  398.7 7.4 %reshape.167 = bf16[2048,8,64]{2,1,0:T(8,128)(2,1)} reshape(bf16[8,2,65536]{2,1,0:T(2,128)(2,1)} %all_to_all.90) | data formatting | bytes 4194304
  406.1 4.5 %copy.39 = bf16[8,256,8,64]{1,3,2,0:T(8,128)(2,1)S(1)} copy(bf16[8,256,8,64]{3,0,1,2:T(8,128)(2,1)} %bitcast.148) | data formatting | bytes 4194304 | tf_op jit(solution)/shard_map/all_to_all | solution.py:73
  410.5 2.4 copy.40
  (80 shorter events, 48.1 us)
Async XLA Ops:
  1.3 14.0 %all-to-all-start.1 = ((bf16[8,256,8]{1,0,2:T(8,128)(2,1)}), bf16[8,256,8]{1,0,2:T(8,128)(2,1)S(1)}, u32[]{:S(2)}, u32[]{:S(2)}) async-start(bf16[8,256,8]{1,0,2:T(8,128)(2,1)} %broadcast_in_dim.23), calls=%async_computation.1 | async-start | bytes 65536 | tf_op jit(solution)/shard_map/all_to_all | solution.py:59
  15.9 10.0 %all-to-all-start.2 = ((bf16[8,256,8]{1,0,2:T(8,128)(2,1)}), bf16[8,256,8]{1,0,2:T(8,128)(2,1)S(1)}, u32[]{:S(2)}, u32[]{:S(2)}) async-start(bf16[8,256,8]{1,0,2:T(8,128)(2,1)} %broadcast_in_dim.24), calls=%async_computation.2 | async-start | bytes 65536 | tf_op jit(solution)/shard_map/all_to_all | solution.py:60
  25.9 50.4 %all-to-all-start = ((bf16[8,256,512]{1,0,2:T(8,128)(2,1)}), bf16[8,256,512]{1,0,2:T(8,128)(2,1)S(1)}, u32[]{:S(2)}, u32[]{:S(2)}) async-start(bf16[8,256,512]{1,0,2:T(8,128)(2,1)} %copy.25), calls=%async_computation | async-start | bytes 4194304 | tf_op jit(solution)/shard_map/all_to_all | solution.py:58
  76.3 52.0 %all-to-all-start.3 = ((bf16[8,256,512]{1,0,2:T(8,128)(2,1)}), bf16[8,256,512]{1,0,2:T(8,128)(2,1)}, u32[]{:S(2)}, u32[]{:S(2)}) async-start(bf16[8,256,512]{1,0,2:T(8,128)(2,1)} %copy.28), calls=%async_computation.3 | async-start | bytes 4194304 | tf_op jit(solution)/shard_map/all_to_all | solution.py:56
  128.3 52.2 %all-to-all-start.4 = ((bf16[8,256,512]{1,0,2:T(8,128)(2,1)}), bf16[8,256,512]{1,0,2:T(8,128)(2,1)}, u32[]{:S(2)}, u32[]{:S(2)}) async-start(bf16[8,256,512]{1,0,2:T(8,128)(2,1)} %copy.31), calls=%async_computation.4 | async-start | bytes 4194304 | tf_op jit(solution)/shard_map/all_to_all | solution.py:57
  141.3 44.2 %copy-start.1 = (bf16[8,2048,64]{1,2,0:T(8,128)(2,1)S(1)}, bf16[8,2048,64]{1,2,0:T(8,128)(2,1)}, u32[]{:S(2)}) copy-start(bf16[8,2048,64]{1,2,0:T(8,128)(2,1)} %custom-call) | copy-start | bytes 6291460
  191.2 3.9 copy-start
  210.0 3.9 copy-start
  228.9 3.9 copy-start
  247.7 3.9 copy-start
  266.6 3.9 copy-start
  285.4 3.9 copy-start
  304.2 3.9 copy-start
  323.1 3.9 copy-start
where the time goes:
time: 415 us; the launch traced here: 413 us
  waiting for transfers between devices  133 us (32%)
  matrix products  122 us (29%)
  local copies, waits for them, and re-layouts  54 us (13%)
  blocking collectives  51.8 us (12%)
  other arithmetic  29 us (7%)
  starting transfers between devices  23.1 us (6%)
    dot_general x32, matrix products, attend_dense(): jnp.einsum('qhd,khd->hqk', query_heads[offset:offset + query_span], key_h...  75.9 us
    all_to_all x1, blocking collectives, local(): lax.all_to_all(shortened(attended), 'seq', split_axis=1, concat_axis=2, t...  51.8 us
    dot_general x32, matrix products, attend_dense(): jnp.einsum('hqk,khd->qhd', weights, value_heads, preferred_element_type=j...  45.9 us
    all_to_all x1, waiting for transfers between devices, local(): lax.all_to_all(queries, 'seq', split_axis=2, concat_axis=1, tiled=True)  43.1 us
    all_to_all x1, waiting for transfers between devices, local(): lax.all_to_all(enc_values, 'seq', split_axis=2, concat_axis=1, tiled=True)  42.1 us
    all_to_all x1, waiting for transfers between devices, local(): lax.all_to_all(enc_keys, 'seq', split_axis=2, concat_axis=1, tiled=True)  39.2 us
    reduce_sum x8, other arithmetic, attend_dense(): row_total = jnp.sum(expos, axis=2, keepdims=True)  27.4 us
    unnamed x7, local copies, waits for them, and re-layouts  27.3 us
  transfers between devices with their start and end apart: 5, of which 5 were waited for; matrix products, arithmetic and copies ran while one was open for 6% of the time, Pallas kernels for 0%

commit v1 on v0

v1 whole, which is shorter than its diff:
```python
import functools
import jax
import jax.numpy as jnp
from jax import lax
from jax.experimental import pallas as pl
from jax.experimental.pallas import tpu as pltpu
from jax.sharding import Mesh, PartitionSpec as P

HEAD_DIM = 64
NDOC = 16
LANES = 2 * HEAD_DIM
BLOCK = 64
CHUNK = 4
NEG = -1.0e30
CLASSES = ((0.4375, 0.09375, 0.015625), (0.53125, 0.15625, 0.015625), (0.625, 0.1875, 0.03125))
FORCE = None


def halves():
    lane = lax.broadcasted_iota(jnp.int32, (1, LANES), 1)
    low = jnp.where(lane < HEAD_DIM, 1.0, 0.0)
    return low.astype(jnp.bfloat16), (1.0 - low).astype(jnp.bfloat16)


def interleave(a, b):
    first = jnp.concatenate([a[:, :HEAD_DIM], b[:, :HEAD_DIM]], axis=1)
    second = jnp.concatenate([a[:, HEAD_DIM:], b[:, HEAD_DIM:]], axis=1)
    return first, second


def pack_pair_kernel(k_ref, v_ref, out_ref):
    for j in range(k_ref.shape[2] // LANES):
        cols = slice(j * LANES, (j + 1) * LANES)
        first, second = interleave(k_ref[0, :, cols], v_ref[0, :, cols])
        out_ref[2 * j, 0] = first
        out_ref[2 * j + 1, 0] = second


def pack_pair(keys, values):
    rows, span, inner = keys.shape
    heads = inner // HEAD_DIM
    return pl.pallas_call(
        pack_pair_kernel,
        grid=(rows,),
        in_specs=[pl.BlockSpec((1, span, inner), lambda r: (r, 0, 0))] * 2,
        out_specs=pl.BlockSpec((heads, 1, span, LANES), lambda r: (0, r, 0, 0)),
        out_shape=jax.ShapeDtypeStruct((heads, rows, span, LANES), keys.dtype),
        cost_estimate=pl.CostEstimate(
            flops=keys.size * 16, bytes_accessed=keys.size * 8, transcendentals=0
        ),
        name="pack_kv",
    )(keys, values)


def pack_queries_kernel(q_ref, out_ref):
    tile = out_ref.shape[2]
    for j in range(q_ref.shape[2] // LANES):
        cols = slice(j * LANES, (j + 1) * LANES)
        first, second = interleave(q_ref[0, :tile, cols], q_ref[0, tile:, cols])
        out_ref[2 * j, 0] = first
        out_ref[2 * j + 1, 0] = second


def pack_queries(queries):
    rows, span, inner = queries.shape
    heads = inner // HEAD_DIM
    return pl.pallas_call(
        pack_queries_kernel,
        grid=(rows,),
        in_specs=[pl.BlockSpec((1, span, inner), lambda r: (r, 0, 0))],
        out_specs=pl.BlockSpec((heads, 1, span // 2, LANES), lambda r: (0, r, 0, 0)),
        out_shape=jax.ShapeDtypeStruct((heads, rows, span // 2, LANES), queries.dtype),
        cost_estimate=pl.CostEstimate(
            flops=queries.size * 16, bytes_accessed=queries.size * 4, transcendentals=0
        ),
        name="pack_q",
    )(queries)


def unpack_kernel(o_ref, out_ref):
    tile = o_ref.shape[2]
    for j in range(out_ref.shape[2] // LANES):
        cols = slice(j * LANES, (j + 1) * LANES)
        top, bottom = interleave(o_ref[2 * j, 0], o_ref[2 * j + 1, 0])
        out_ref[0, :tile, cols] = top
        out_ref[0, tile:, cols] = bottom


def unpack(outputs):
    heads, rows, tile, _ = outputs.shape
    inner = heads * HEAD_DIM
    return pl.pallas_call(
        unpack_kernel,
        grid=(rows,),
        in_specs=[pl.BlockSpec((heads, 1, tile, LANES), lambda r: (0, r, 0, 0))],
        out_specs=pl.BlockSpec((1, 2 * tile, inner), lambda r: (r, 0, 0)),
        out_shape=jax.ShapeDtypeStruct((rows, 2 * tile, inner), outputs.dtype),
        cost_estimate=pl.CostEstimate(
            flops=outputs.size * 16, bytes_accessed=outputs.size * 4, transcendentals=0
        ),
        name="unpack_o",
    )(outputs)


class Sizes:
    def __init__(self, mesh_shape, batch, length, inner):
        self.heads = inner // HEAD_DIM
        self.dp = mesh_shape["dp"]
        self.x = self.heads // self.dp
        self.z = mesh_shape["seq"] // self.x
        self.rows = batch
        self.own_rows = batch // self.dp
        self.length = length
        self.span = length // (self.x * self.z)
        self.level = length // self.z
        self.tile = self.span // 2
        self.part_blocks = self.span // BLOCK
        self.level_blocks = self.level // BLOCK
        self.shifts = [s for s in range(-(self.z - 1), self.z) if s]


def spans(sz, counts):
    total = counts.sum(axis=(1, 2)).reshape(sz.rows, 2, NDOC)
    before = jnp.arange(NDOC)[:, None] > jnp.arange(NDOC)[None, :]
    start = jnp.where(before, total[:, :, None, :], 0).sum(axis=3)
    end = start + total
    dec_start, enc_start = start[:, 0], start[:, 1]
    dec_end, enc_end = end[:, 0], end[:, 1]
    first = jnp.arange(sz.z * sz.x)[None, :, None] * sz.span
    last = first + sz.span - 1
    holds = lambda at: (dec_start[:, None] <= at) & (at < dec_end[:, None])
    low = jnp.where(holds(first), enc_start[:, None], 0).sum(axis=2) // BLOCK
    high = (jnp.where(holds(last), enc_end[:, None], 0).sum(axis=2) + BLOCK - 1) // BLOCK
    low, high = low.reshape(sz.rows, sz.z, sz.x), high.reshape(sz.rows, sz.z, sz.x)
    return (dec_start, dec_end, enc_start, enc_end), low, high


def tables(sz, docs, low, high):
    me = lax.axis_index("z")
    need_low, need_high = low[:, :, 0], high[:, :, -1]
    level = jnp.arange(sz.z) * sz.level_blocks
    run_low = jnp.maximum(need_low[:, None, :], level[None, :, None])
    run_high = jnp.minimum(need_high[:, None, :], level[None, :, None] + sz.level_blocks)
    count = jnp.maximum(run_high - run_low, 0)
    earlier = jnp.arange(sz.rows)[:, None] > jnp.arange(sz.rows)[None, :]
    offset = jnp.where(earlier[:, :, None, None], count[None], 0).sum(axis=1)
    sums = count.sum(axis=0)
    gap = jnp.arange(sz.z)[None, :] - jnp.arange(sz.z)[:, None]
    worst = [jnp.where(gap == s, sums, 0).max() for s in sz.shifts]

    shifts = jnp.arange(-(sz.z - 1), sz.z)
    here = jnp.arange(sz.z) == me
    into = (gap[None] == shifts[:, None, None]) & here[None, None, :]
    out_of = (gap[None] == shifts[:, None, None]) & here[None, :, None]
    pick = lambda sel, v: jnp.where(sel[None], v[:, None], 0).sum(axis=(2, 3))
    receive = jnp.stack([pick(into, count), pick(into, offset), pick(into, run_low)])
    send = jnp.stack([pick(out_of, count), pick(out_of, offset), pick(out_of, run_low)])
    mine = lambda v: jnp.where(here[None, :, None], v, 0).sum(axis=1)
    unit_low, unit_high = mine(low), mine(high)
    base = unit_low[:, :1]
    units = jnp.concatenate([base, unit_high[:, -1:], unit_low, unit_high], axis=1)

    dec_start, dec_end, enc_start, enc_end = docs
    ahead = jnp.zeros((sz.rows, HEAD_DIM), jnp.int32)
    rest = LANES - HEAD_DIM - NDOC
    open_low = jnp.zeros((sz.rows, rest), jnp.int32)
    open_high = jnp.full((sz.rows, rest), 1 << 30, jnp.int32)
    row_of = lambda v, fill: jnp.concatenate([ahead, v, fill], axis=1)
    lanes = jnp.stack(
        [row_of(enc_start, open_low), row_of(enc_end, open_high),
         row_of(dec_start, open_low), row_of(dec_end, open_high)], axis=1,
    )
    return receive, send, units, lanes, worst


def select_kernel(sz, send_ref, me_ref, kv_ref, *out_refs):
    per = sz.own_rows * sz.part_blocks
    first = me_ref[0] * sz.level_blocks
    shifts = 2 * sz.z - 1
    for out_ref, shift in zip(out_refs, sz.shifts):
        slot = shift + sz.z - 1

        @pl.loop(0, sz.rows)
        def _(row):
            at = row * shifts + slot
            count, offset = send_ref[0, at], send_ref[1, at]
            low = send_ref[2, at] - first
            base = (row // sz.own_rows) * (sz.x * per) + (row % sz.own_rows) * sz.part_blocks

            @pl.loop(0, count)
            def _(i):
                block = low + i
                source = base + (block // sz.part_blocks) * per + block % sz.part_blocks
                out_ref[offset + i] = kv_ref[source]


def select_blocks(sz, caps, send, me, kv):
    size = sum(caps) * BLOCK * LANES * 2
    return pl.pallas_call(
        functools.partial(select_kernel, sz),
        in_specs=[pl.BlockSpec(memory_space=pltpu.SMEM)] * 2
        + [pl.BlockSpec(memory_space=pltpu.VMEM)],
        out_specs=[pl.BlockSpec(memory_space=pltpu.VMEM)] * len(caps),
        out_shape=[jax.ShapeDtypeStruct((cap, BLOCK, LANES), kv.dtype) for cap in caps],
        cost_estimate=pl.CostEstimate(flops=size, bytes_accessed=2 * size, transcendentals=0),
        name="select_blocks",
    )(send, me, kv)


def attend_kernel(sz, group, whole, receive_ref, units_ref, me_ref, lanes_ref, q_ref, kv_ref, *refs):
    sources = len(sz.shifts)
    others, (o_ref, k_scr, v_scr, s_scr, m_scr, a_scr) = refs[:sources], refs[sources:]
    low_mask, high_mask = halves()
    shifts = 2 * sz.z - 1
    per = sz.own_rows * sz.part_blocks
    me = me_ref[0]
    dp, step = pl.program_id(0), pl.program_id(1)
    width = 2 + 2 * sz.x
    first_row = dp * sz.own_rows + step * group
    position = lax.broadcasted_iota(jnp.int32, (BLOCK, LANES), 0)

    def unit(g, x):
        at = (first_row + g) * width
        base = units_ref[at]
        return units_ref[at + 2 + x] - base, units_ref[at + 2 + sz.x + x] - base

    chunks = 1
    for g in range(group):
        for x in range(sz.x):
            begin, end = unit(g, x)
            chunks = jnp.maximum(chunks, (end - begin + CHUNK - 1) // CHUNK)

    for g in range(group):
        row = first_row + g
        base, stop = units_ref[row * width], units_ref[row * width + 1]
        enc_start, enc_end = lanes_ref[0, g, 0:1, :], lanes_ref[0, g, 1:2, :]

        def put(block, kv, g=g, base=base, enc_start=enc_start, enc_end=enc_end):
            at = pl.multiple_of((block - base) * BLOCK, BLOCK)
            where = position + block * BLOCK
            inside = (where >= enc_start) & (where < enc_end)
            mask = jnp.where(inside, 0.0, NEG).astype(jnp.bfloat16) * high_mask
            k_scr[g, pl.ds(at, BLOCK), :] = kv * low_mask + mask
            v_scr[g, pl.ds(at, BLOCK), :] = kv * high_mask + low_mask

        for slot in range(shifts):
            at = row * shifts + slot
            count, offset, low = receive_ref[0, at], receive_ref[1, at], receive_ref[2, at]
            shift = slot - (sz.z - 1)
            in_level = low - (me - shift) * sz.level_blocks

            @pl.loop(0, count)
            def _(i, slot=slot, shift=shift, offset=offset, low=low, in_level=in_level, put=put, g=g):
                block = in_level + i
                part, inner = block // sz.part_blocks, block % sz.part_blocks
                if shift == 0:
                    row_base = dp * (sz.x * per) + (step * group + g) * sz.part_blocks
                    kv = kv_ref[row_base + part * per + inner]
                elif whole:
                    kv = others[sz.shifts.index(shift)][0, part, g, inner]
                else:
                    kv = others[sz.shifts.index(shift)][offset + i]
                put(low + i, kv)

        tail = chunks * CHUNK
        last = 0
        for x in range(sz.x):
            last = jnp.maximum(last, unit(g, x)[0] + tail)

        @pl.loop(stop - base, last)
        def _(i, g=g):
            at = pl.multiple_of(i * BLOCK, BLOCK)
            k_scr[g, pl.ds(at, BLOCK), :] = jnp.broadcast_to(
                (high_mask * NEG).astype(jnp.bfloat16), (BLOCK, LANES)
            )
            v_scr[g, pl.ds(at, BLOCK), :] = jnp.zeros((BLOCK, LANES), jnp.bfloat16)

    pieces = [(g, x, h) for g in range(group) for x in range(sz.x) for h in range(2)]
    q_position = lax.broadcasted_iota(jnp.int32, (sz.tile, LANES), 0)
    asked = []
    for g, x, h in pieces:
        where = q_position + (me * sz.level + x * sz.span + h * sz.tile)
        inside = (where >= lanes_ref[0, g, 2:3, :]) & (where < lanes_ref[0, g, 3:4, :])
        hot = jnp.where(inside, 1.0, 0.0).astype(jnp.bfloat16) * high_mask
        q = q_ref[0, x, g]
        if h:
            q = pltpu.roll(q.astype(jnp.float32), HEAD_DIM, 1).astype(jnp.bfloat16)
        asked.append(q * low_mask + hot)

    for n in range(len(pieces)):
        m_scr[n] = jnp.full((sz.tile, LANES), -3.0e38, jnp.float32)
        a_scr[n] = jnp.zeros((sz.tile, LANES), jnp.float32)
    keys = CHUNK * BLOCK

    def at_chunk(g, x, c):
        return pl.ds(pl.multiple_of((unit(g, x)[0] + c * CHUNK) * BLOCK, BLOCK), keys)

    @pl.loop(0, chunks)
    def _(c):
        for n, (g, x, h) in enumerate(pieces):
            k = k_scr[g, at_chunk(g, x, c), :]
            s = lax.dot_general(
                asked[n], k, (((1,), (1,)), ((), ())), preferred_element_type=jnp.float32
            )
            s_scr[n, c] = s
            peak = m_scr[n]
            for j in range(0, keys, LANES):
                peak = jnp.maximum(peak, s[:, j : j + LANES])
            m_scr[n] = peak

    for n in range(len(pieces)):
        peak = jnp.max(m_scr[n], axis=1, keepdims=True)
        m_scr[n] = jnp.broadcast_to(peak, (sz.tile, LANES))

    @pl.loop(0, chunks)
    def _(c):
        for n, (g, x, h) in enumerate(pieces):
            peak = m_scr[n]
            s = s_scr[n, c]
            p = jnp.concatenate(
                [jnp.exp(s[:, j : j + LANES] - peak) for j in range(0, keys, LANES)], axis=1
            ).astype(jnp.bfloat16)
            v = v_scr[g, at_chunk(g, x, c), :]
            a_scr[n] += jnp.dot(p, v, preferred_element_type=jnp.float32)

    lane = lax.broadcasted_iota(jnp.int32, (sz.tile, LANES), 1)
    for n in range(0, len(pieces), 2):
        g, x, _ = pieces[n]
        first, second = a_scr[n], a_scr[n + 1]
        top = jnp.where(lane < HEAD_DIM, pltpu.roll(first, HEAD_DIM, 1), second)
        bottom = jnp.where(lane < HEAD_DIM, first, pltpu.roll(second, HEAD_DIM, 1))
        o_ref[0, x, g] = (top / bottom).astype(o_ref.dtype)


def attend(sz, whole, receive, units, me, lanes, q, kv, others):
    group = 2
    tile, blocks = sz.tile, sz.length // BLOCK
    room = 2 * blocks + CHUNK
    pieces = group * sz.x * 2
    lanes = lanes.reshape(sz.dp, sz.own_rows, 4, LANES)
    kv_spec = pl.BlockSpec(memory_space=pltpu.VMEM)
    if whole:
        other_spec = pl.BlockSpec(
            (1, sz.x, group, sz.part_blocks, BLOCK, LANES), lambda d, r, *_: (d, 0, r, 0, 0, 0)
        )
        others = [
            o.reshape(sz.dp, sz.x, sz.own_rows, sz.part_blocks, BLOCK, LANES) for o in others
        ]
    else:
        other_spec = kv_spec
    io_spec = pl.BlockSpec((1, sz.x, group, tile, LANES), lambda d, r, *_: (d, 0, r, 0, 0))
    most = -(-blocks // CHUNK)
    return pl.pallas_call(
        functools.partial(attend_kernel, sz, group, whole),
        grid_spec=pltpu.PrefetchScalarGridSpec(
            num_scalar_prefetch=3,
            grid=(sz.dp, sz.own_rows // group),
            in_specs=[
                pl.BlockSpec((1, group, 4, LANES), lambda d, r, *_: (d, r, 0, 0)),
                io_spec,
                kv_spec,
            ]
            + [other_spec] * len(others),
            out_specs=io_spec,
            scratch_shapes=[
                pltpu.VMEM((group, room * BLOCK, LANES), jnp.bfloat16),
                pltpu.VMEM((group, room * BLOCK, LANES), jnp.bfloat16),
                pltpu.VMEM((pieces, most, tile, CHUNK * BLOCK), jnp.float32),
                pltpu.VMEM((pieces, tile, LANES), jnp.float32),
                pltpu.VMEM((pieces, tile, LANES), jnp.float32),
            ],
        ),
        out_shape=jax.ShapeDtypeStruct((sz.dp, sz.x, sz.own_rows, tile, LANES), q.dtype),
        cost_estimate=pl.CostEstimate(
            flops=sz.rows * sz.level * 512 * 512,
            bytes_accessed=4 * q.size + 4 * kv.size,
            transcendentals=sz.rows * sz.level * 512,
        ),
        name="attend",
    )(receive, units, me, lanes, q, kv, *others)


def local(sz, queries, enc_keys, enc_values, dec_ids, enc_ids):
    plane = ("dp", "x")
    devices = sz.dp * sz.z * sz.x
    numbers = jnp.stack([dec_ids, enc_ids], axis=1)
    counts = (numbers[..., None] == jnp.arange(NDOC)).astype(jnp.int32).sum(axis=2)
    counts = counts.reshape(sz.own_rows, 2 * NDOC)
    counts = lax.all_to_all(
        jnp.broadcast_to(counts[None], (devices,) + counts.shape),
        ("dp", "z", "x"), split_axis=0, concat_axis=0, tiled=True,
    ).reshape(sz.dp, sz.z, sz.x, sz.own_rows, 2 * NDOC)
    docs, low, high = spans(sz, counts)
    receive, send, units, lanes, worst = tables(sz, docs, low, high)
    me = lax.axis_index("z").reshape(1).astype(jnp.int32)
    flat = lambda v: v.reshape(3, -1)

    blocks = sz.rows * sz.level_blocks
    classes = []
    for shares in CLASSES:
        classes.append([int(blocks * shares[min(abs(s), len(shares)) - 1]) for s in sz.shifts])
    index = sum(
        (~functools.reduce(lambda a, b: a & b, [w <= c for w, c in zip(worst, caps)])).astype(jnp.int32)
        for caps in classes
    )
    if FORCE is not None:
        index = jnp.int32(FORCE)

    kv_packed = pack_pair(enc_keys, enc_values)
    q_packed = pack_queries(queries)

    def run(caps, args):
        kv_packed, q_packed, receive, send, units, lanes, me = args
        kv = lax.all_to_all(kv_packed, plane, split_axis=0, concat_axis=0, tiled=True)
        kv = kv.reshape(-1, BLOCK, LANES)
        if caps is None:
            sent = [kv] * len(sz.shifts)
        else:
            sent = select_blocks(sz, caps, flat(send), me, kv)
        others = []
        for buffer, shift in zip(sent, sz.shifts):
            pairs = [(i, i + shift) for i in range(sz.z) if 0 <= i + shift < sz.z]
            others.append(lax.ppermute(buffer, "z", pairs))
        q = lax.all_to_all(q_packed, plane, split_axis=0, concat_axis=0, tiled=True)
        q = q.reshape(sz.dp, sz.x, sz.own_rows, sz.tile, LANES)
        out = attend(
            sz, caps is None, flat(receive), units.reshape(-1), me, lanes, q, kv, others
        )
        out = out.reshape(sz.dp * sz.x, sz.own_rows, sz.tile, LANES)
        out = lax.all_to_all(out, plane, split_axis=0, concat_axis=0, tiled=True)
        return unpack(out)

    args = (kv_packed, q_packed, receive, send, units, lanes, me)
    return lax.switch(index, [functools.partial(run, caps) for caps in classes + [None]], args)


def solution(mesh):
    def whole(queries, enc_keys, enc_values, dec_ids, enc_ids):
        batch, length, inner = queries.shape
        sz = Sizes(mesh.shape, batch, length, inner)
        fine = Mesh(mesh.devices.reshape(sz.dp, sz.z, sz.x), ("dp", "z", "x"))
        wide, narrow = P("dp", ("z", "x"), None), P("dp", ("z", "x"))
        return jax.shard_map(
            functools.partial(local, sz), mesh=fine,
            in_specs=(wide, wide, wide, narrow, narrow), out_specs=wide, check_vma=False,
        )(queries, enc_keys, enc_values, dec_ids, enc_ids)

    return whole
```

time: 415 us -> 280 us (0.67)
  matrix products: 122 us -> 0 us
  Pallas kernels: 0 us -> 85.7 us
  local copies, waits for them, and re-layouts: 54 us -> 5.78 us
  waiting for transfers between devices: 133 us -> 107 us
  other arithmetic: 29 us -> 4 us
  blocking collectives: 51.8 us -> 30.3 us
  starting transfers between devices: 23.1 us -> 35.1 us
  between operations: 0.08 us -> 10.2 us
    dot_general x64 -> x0, matrix products: 122 us -> none  [the longest x32 75.9 us: attend_dense(): jnp.einsum('qhd,khd->hqk', query_heads[offset:offset + query_span], key_h...]
    pallas_call x0 -> x5, Pallas kernels: none -> 85.7 us  [the longest x1 58.3 us: attend(): pl.pallas_call(functools.partial(attend_kernel, sz, group, whole), grid_s...]
    all_to_all x5 -> x3, waiting for transfers between devices: 133 us -> 47.7 us  [the longest x1 47.7 us: run(): lax.all_to_all(kv_packed, plane, split_axis=0, concat_axis=0, tiled=True)]
    ppermute x0 -> x6, waiting for transfers between devices: none -> 58.8 us  [run(): others.append(lax.ppermute(buffer, 'z', pairs))]
    reduce_sum x8 -> x7, other arithmetic: 27.4 us -> 1.28 us  [the longest x1 0.37 us: local(): (numbers[..., None] == jnp.arange(NDOC)).astype(jnp.int32).sum(axis=2)]
    unnamed x7 -> x4, local copies, waits for them, and re-layouts: 27.3 us -> 2.11 us
    all_to_all x1, blocking collectives: 51.8 us -> 30.3 us  [run(): out = lax.all_to_all(out, plane, split_axis=0, concat_axis=0, tiled=True)]
    ppermute x0 -> x6, starting transfers between devices: none -> 19.4 us  [run(): others.append(lax.ppermute(buffer, 'z', pairs))]
  transfers between devices with their start and end apart: 5 -> 9, of which waited for: 5 -> 3; matrix products, arithmetic and copies ran while one was open for 6% -> 1% of each run, Pallas kernels for 0% -> 5%
where the time goes in v1:
time: 280 us; the launch traced here: 278 us
  waiting for transfers between devices  107 us (38%)
  Pallas kernels  85.7 us (31%)
  starting transfers between devices  35.1 us (13%)
  blocking collectives  30.3 us (11%)
  between operations  10.2 us (4%)
  local copies, waits for them, and re-layouts  5.78 us (2%)
  other arithmetic  4 us (1%)
    ppermute x6, waiting for transfers between devices, run(): others.append(lax.ppermute(buffer, 'z', pairs))  58.8 us
    pallas_call x1, Pallas kernels, attend(): pl.pallas_call(functools.partial(attend_kernel, sz, group, whole), grid_s...  58.3 us
    all_to_all x1, waiting for transfers between devices, run(): lax.all_to_all(kv_packed, plane, split_axis=0, concat_axis=0, tiled=True)  47.7 us
    all_to_all x1, blocking collectives, run(): out = lax.all_to_all(out, plane, split_axis=0, concat_axis=0, tiled=True)  30.3 us
    ppermute x6, starting transfers between devices, run(): others.append(lax.ppermute(buffer, 'z', pairs))  19.4 us
    pallas_call x1, Pallas kernels, select_blocks(): pl.pallas_call(functools.partial(select_kernel, sz), in_specs=[pl.BlockSp...  9.56 us
    all_to_all x1, starting transfers between devices, local(): lax.all_to_all(jnp.broadcast_to(counts[None], (devices,) + counts.shape),...  7.33 us
    pallas_call x1, Pallas kernels, pack_pair(): pl.pallas_call(pack_pair_kernel, grid=(rows,), in_specs=[pl.BlockSpec((1,...  7.17 us
  transfers between devices with their start and end apart: 9, of which 3 were waited for; matrix products, arithmetic and copies ran while one was open for 1% of the time, Pallas kernels for 5%

profile of v1, /device:TPU:0, one launch (start us, length us, event | category | flops | bytes accessed | tf_op | source)
XLA Modules:
  0.0 278.0 jit_solution(919592037054679719)
XLA Ops:
  0.0 0.7 pad_add_fusion.1
  0.7 0.4 convert_reduce_fusion
  1.1 0.1 broadcast_in_dim.194
  1.2 0.7 reshape.184
  1.9 7.3 %all-to-all-start.12 = ((s32[32,1,256]{2,1,0:T(1,128)}), s32[32,1,256]{2,1,0:T(1,128)S(1)}, u32[]{:S(2)}, u32[]{:S(2)}) async-start(s32[32,1,256]{2,1,0:T(1,128)} %reshape.184), calls=%async_computation.12 | async-start | bytes 65536 | tf_op jit(solution)/shard_map/all_to_all | solution.py:389
  9.3 0.1 pad.18.clone
  9.4 0.1 pad.15.clone
  9.5 6.0 %pack_q.1 = bf16[8,8,128,128]{3,2,1,0:T(8,128)(2,1)} custom-call(bf16[8,256,512]{2,1,0:T(8,128)(2,1)} %q_ref.1), custom_call_target="tpu_custom_call" | custom-call | flops 16777216 | bytes 4194304 | tf_op jit(solution)/shard_map/pack_q/pallas_call | solution.py:67
  15.5 7.2 %pack_kv.1 = bf16[8,8,256,128]{3,2,1,0:T(8,128)(2,1)} custom-call(bf16[8,256,512]{2,1,0:T(8,128)(2,1)} %k_ref.1, bf16[8,256,512]{2,1,0:T(8,128)(2,1)} %v_ref.1), custom_call_target="tpu_custom_call" | custom-call | flops 16777216 | bytes 8388608 | tf_op jit(solution)/shard_map/pack_kv/pallas_call | solution.py:42
  22.7 0.1 compare_and_fusion.1
  22.8 0.0 all-to-all-done.12
  22.8 0.5 broadcast.230
  23.3 0.7 reduce
  24.0 0.1 reshape.185
  24.1 0.1 broadcast_in_dim.196
  24.2 0.1 copy.41
  24.3 0.1 select_reduce_fusion.1
  24.5 0.1 copy.43
  24.6 0.1 copy.45
  24.6 0.1 copy.46
  24.7 0.1 copy.44
  24.8 0.1 select_reduce_fusion.3
  24.9 0.1 select_reduce_fusion.11
  25.0 0.2 subtract_maximum_fusion
  25.2 0.8 select_reduce_fusion.12
  36.0 0.4 select_reduce_fusion
  36.4 0.2 select_reduce_fusion.4
  36.6 0.1 add_add_fusion
  36.7 0.1 pad_add_fusion
  36.8 239.9 %conditional.1 = (bf16[8,256,512]{2,1,0:T(8,128)(2,1)S(1)}) conditional(s32[]{:T(128)} %clamp.3, (s32[3,32,7]{1,2,0:T(8,128)S(1)}, s32[32,6]{0,1:T(8,128)S(1)}, s32[32,4,128]{2,1,0:T(4,128)S(1)}, bf16[8,8,128,128]{3,2,1,0:T(8,128)(2,1)}, bf16[8,8,256,128]{3,2,1,0:T(8,128)(2,1)}, /*index=5*/s32[3,32,7]{1,2,0:T(8,128)S(1)}, ...), branch_computations={%region_21.22_spmd, %region_22.23_spmd, %region_23.24_spmd, %regio... | conditional | flops 4318822400 | bytes 144717600 | solution.py:434
  36.8 4.6 %all-to-all-start.4 = ((bf16[8,8,256,128]{3,2,1,0:T(8,128)(2,1)}), bf16[8,8,256,128]{3,2,1,0:T(8,128)(2,1)}, u32[]{:S(2)}, u32[]{:S(2)}) async-start(bf16[8,8,256,128]{3,2,1,0:T(8,128)(2,1)} %get-tuple-element.82), calls=%async_computation.4 | async-start | bytes 8388608 | tf_op jit(solution)/shard_map/cond/branch_1_fun/all_to_all | solution.py:414
  41.4 0.1 copy.55
  41.5 0.7 reshape.159.send_ref
  42.2 47.7 %all-to-all-done.4 = bf16[8,8,256,128]{3,2,1,0:T(8,128)(2,1)} async-done(((bf16[8,8,256,128]{3,2,1,0:T(8,128)(2,1)}), bf16[8,8,256,128]{3,2,1,0:T(8,128)(2,1)}, u32[]{:S(2)}, u32[]{:S(2)}) %all-to-all-start.4) | async-done | bytes 4194336 | tf_op jit(solution)/shard_map/cond/branch_1_fun/all_to_all | solution.py:414
  89.9 9.6 %select_blocks.4 = (bf16[4,64,128]{2,1,0:T(8,128)(2,1)}, bf16[40,64,128]{2,1,0:T(8,128)(2,1)}, bf16[136,64,128]{2,1,0:T(8,128)(2,1)}, bf16[136,64,128]{2,1,0:T(8...) custom-call(s32[3,224]{1,0:T(4,128)} %reshape.159.send_ref, s32[1]{0:T(128)} %get-tuple-element.79.me_ref, ...), custom_call_target="tpu_custom_call" | custom-call | flops 5898240 | bytes 11796480 | tf_op jit(solution)/shard_map/cond/branch_1_fun/select_blocks/pallas_call | solution.py:199
  99.5 1.3 collective-permute-start.8
  100.8 6.3 %collective-permute-start.9 = (bf16[136,64,128]{2,1,0:T(8,128)(2,1)}, bf16[136,64,128]{2,1,0:T(8,128)(2,1)}, u32[]{:S(2)}, u32[]{:S(2)}) collective-permute-start(bf16[136,64,128]{2,1,0:T(8,128)(2,1)} %get-tuple-element.87), channel_id=1, source_target_pairs={{0,2},{2,4},{4,6},{1,3},{3,5},{5,7},{8,10},{10,12},{12,14},{9,11},... | collective-permute-start | bytes 6684680 | tf_op jit(solution)/shard_map/cond/branch_1_fun/ppermute | solution.py:423
  107.1 0.0 copy-start.7
  107.1 0.0 copy-start.6
  107.1 3.7 %all-to-all-start.3 = ((bf16[8,8,128,128]{3,2,1,0:T(8,128)(2,1)}), bf16[8,8,128,128]{3,2,1,0:T(8,128)(2,1)S(1)}, u32[]{:S(2)}, u32[]{:S(2)}) async-start(bf16[8,8,128,128]{3,2,1,0:T(8,128)(2,1)} %get-tuple-element.81), calls=%async_computation.3 | async-start | bytes 4194304 | tf_op jit(solution)/shard_map/cond/branch_1_fun/all_to_all | solution.py:424
  110.9 0.0 copy-done.7
  110.9 1.3 collective-permute-start.7
  112.2 0.0 copy-done.6
  112.2 7.1 %collective-permute-start.10 = (bf16[40,64,128]{2,1,0:T(8,128)(2,1)S(1)}, bf16[40,64,128]{2,1,0:T(8,128)(2,1)}, u32[]{:S(2)}, u32[]{:S(2)}) collective-permute-start(bf16[40,64,128]{2,1,0:T(8,128)(2,1)S(1)} %copy-done.6), channel_id=1, source_target_pairs={{0,4},{2,6},{1,5},{3,7},{8,12},{10,14},{9,13},{11,15},{16,20},{18,... | collective-permute-start | bytes 1966088 | tf_op jit(solution)/shard_map/cond/branch_1_fun/ppermute | solution.py:423
  119.3 1.3 collective-permute-start.6
  120.6 49.1 %collective-permute-done.6.refs_0_ = bf16[4,64,128]{2,1,0:T(8,128)(2,1)S(1)} collective-permute-done((bf16[4,64,128]{2,1,0:T(8,128)(2,1)}, bf16[4,64,128]{2,1,0:T(8,128)(2,1)S(1)}, u32[]{:S(2)}, u32[]{:S(2)}) %collective-permute-start.6) | collective-permute-done | bytes 65568 | tf_op jit(solution)/shard_map/cond/branch_1_fun/ppermute | solution.py:423
  169.7 2.1 collective-permute-start.11
  171.8 0.0 copy-done.15
  171.8 0.1 copy.54
  171.9 0.7 reshape.155.units_ref
  172.6 0.1 copy.53
  172.7 0.7 reshape.154.receive_ref
  173.4 0.0 all-to-all-done.3
  173.4 0.0 collective-permute-done.11.refs_5_
  173.4 9.8 %collective-permute-done.7.refs_1_ = bf16[40,64,128]{2,1,0:T(8,128)(2,1)} collective-permute-done((bf16[40,64,128]{2,1,0:T(8,128)(2,1)S(1)}, bf16[40,64,128]{2,1,0:T(8,128)(2,1)}, u32[]{:S(2)}, u32[]{:S(2)}) %collective-permute-start.7) | collective-permute-done | bytes 655392 | tf_op jit(solution)/shard_map/cond/branch_1_fun/ppermute | solution.py:423
  183.2 0.0 collective-permute-done.10.refs_4_
  183.2 0.0 collective-permute-done.8.refs_2_
  183.2 0.0 collective-permute-done.9.refs_3_
  183.2 0.0 copy-done.2
  183.2 58.3 %attend.5 = bf16[4,2,8,128,128]{4,3,2,1,0:T(8,128)(2,1)} custom-call(s32[3,224]{1,0:T(4,128)} %reshape.154.receive_ref, s32[192]{0:T(256)} %reshape.155.units_ref, s32[1]{0:T(128)} %get-tuple-element.79.me_ref, s32[4,8,4,128]{3,2,1,0:T(4,128)S(1)} %bitcast.64, bf16[4,2,8,128,128]{4,3,2,1,0:T(8,128)(2,1)} %bitcast.58, bf16[256,64,128]{2,1,0:T(8,128)(2,1)} %bitcast.6.kv_ref, ...), custom_call_target="tpu_custom_call" | custom-call | flops 4294967296 | bytes 12582912 | tf_op jit(solution)/shard_map/cond/branch_1_fun/attend/pallas_call | solution.py:353
  241.5 30.3 %all_to_all.54.o_ref = bf16[8,8,128,128]{3,2,1,0:T(8,128)(2,1)} all-to-all(bf16[8,8,128,128]{3,2,1,0:T(8,128)(2,1)} %bitcast.61), channel_id=1, replica_groups=mesh['dp'=4,'z'=4,'x'=2] {'dp','x'}, dimensions={0} | all-to-all | bytes 4194304 | tf_op jit(solution)/shard_map/cond/branch_1_fun/all_to_all | solution.py:430
  271.9 4.6 %unpack_o.5 = bf16[8,256,512]{2,1,0:T(8,128)(2,1)S(1)} custom-call(bf16[8,8,128,128]{3,2,1,0:T(8,128)(2,1)} %all_to_all.54.o_ref), custom_call_target="tpu_custom_call" | custom-call | flops 16777216 | bytes 4194304 | tf_op jit(solution)/shard_map/cond/branch_1_fun/unpack_o/pallas_call | solution.py:92
  276.7 0.0 copy-start.4
  276.7 1.3 copy-done.4
  (26 shorter events, 0.1 us)
Async XLA Ops:
  1.9 20.9 %all-to-all-start.12 = ((s32[32,1,256]{2,1,0:T(1,128)}), s32[32,1,256]{2,1,0:T(1,128)S(1)}, u32[]{:S(2)}, u32[]{:S(2)}) async-start(s32[32,1,256]{2,1,0:T(1,128)} %reshape.184), calls=%async_computation.12 | async-start | bytes 65536 | tf_op jit(solution)/shard_map/all_to_all | solution.py:389
  36.8 53.1 %all-to-all-start.4 = ((bf16[8,8,256,128]{3,2,1,0:T(8,128)(2,1)}), bf16[8,8,256,128]{3,2,1,0:T(8,128)(2,1)}, u32[]{:S(2)}, u32[]{:S(2)}) async-start(bf16[8,8,256,128]{3,2,1,0:T(8,128)(2,1)} %get-tuple-element.82), calls=%async_computation.4 | async-start | bytes 8388608 | tf_op jit(solution)/shard_map/cond/branch_1_fun/all_to_all | solution.py:414
  99.5 83.7 %collective-permute-start.8 = (bf16[136,64,128]{2,1,0:T(8,128)(2,1)}, bf16[136,64,128]{2,1,0:T(8,128)(2,1)}, u32[]{:S(2)}, u32[]{:S(2)}) collective-permute-start(bf16[136,64,128]{2,1,0:T(8,128)(2,1)} %get-tuple-element.86), channel_id=1, source_target_pairs={{2,0},{4,2},{6,4},{3,1},{5,3},{7,5},{10,8},{12,10},{14,12},{11,9},... | collective-permute-start | bytes 6684680 | tf_op jit(solution)/shard_map/cond/branch_1_fun/ppermute | solution.py:423
  100.8 82.4 %collective-permute-start.9 = (bf16[136,64,128]{2,1,0:T(8,128)(2,1)}, bf16[136,64,128]{2,1,0:T(8,128)(2,1)}, u32[]{:S(2)}, u32[]{:S(2)}) collective-permute-start(bf16[136,64,128]{2,1,0:T(8,128)(2,1)} %get-tuple-element.87), channel_id=1, source_target_pairs={{0,2},{2,4},{4,6},{1,3},{3,5},{5,7},{8,10},{10,12},{12,14},{9,11},... | collective-permute-start | bytes 6684680 | tf_op jit(solution)/shard_map/cond/branch_1_fun/ppermute | solution.py:423
  107.1 3.8 %copy-start.7 = (bf16[40,64,128]{2,1,0:T(8,128)(2,1)S(1)}, bf16[40,64,128]{2,1,0:T(8,128)(2,1)}, u32[]{:S(2)}) copy-start(bf16[40,64,128]{2,1,0:T(8,128)(2,1)} %get-tuple-element.85) | copy-start | bytes 1966084 | tf_op jit(solution)/shard_map/cond
  107.1 5.1 %copy-start.6 = (bf16[40,64,128]{2,1,0:T(8,128)(2,1)S(1)}, bf16[40,64,128]{2,1,0:T(8,128)(2,1)}, u32[]{:S(2)}) copy-start(bf16[40,64,128]{2,1,0:T(8,128)(2,1)} %get-tuple-element.88) | copy-start | bytes 1966084 | tf_op jit(solution)/shard_map/cond
  107.1 66.3 %all-to-all-start.3 = ((bf16[8,8,128,128]{3,2,1,0:T(8,128)(2,1)}), bf16[8,8,128,128]{3,2,1,0:T(8,128)(2,1)S(1)}, u32[]{:S(2)}, u32[]{:S(2)}) async-start(bf16[8,8,128,128]{3,2,1,0:T(8,128)(2,1)} %get-tuple-element.81), calls=%async_computation.3 | async-start | bytes 4194304 | tf_op jit(solution)/shard_map/cond/branch_1_fun/all_to_all | solution.py:424
  110.9 72.3 %collective-permute-start.7 = (bf16[40,64,128]{2,1,0:T(8,128)(2,1)S(1)}, bf16[40,64,128]{2,1,0:T(8,128)(2,1)}, u32[]{:S(2)}, u32[]{:S(2)}) collective-permute-start(bf16[40,64,128]{2,1,0:T(8,128)(2,1)S(1)} %copy-done.7), channel_id=1, source_target_pairs={{4,0},{6,2},{5,1},{7,3},{12,8},{14,10},{13,9},{15,11},{20,16},{22,... | collective-permute-start | bytes 1966088 | tf_op jit(solution)/shard_map/cond/branch_1_fun/ppermute | solution.py:423
  112.2 71.0 %collective-permute-start.10 = (bf16[40,64,128]{2,1,0:T(8,128)(2,1)S(1)}, bf16[40,64,128]{2,1,0:T(8,128)(2,1)}, u32[]{:S(2)}, u32[]{:S(2)}) collective-permute-start(bf16[40,64,128]{2,1,0:T(8,128)(2,1)S(1)} %copy-done.6), channel_id=1, source_target_pairs={{0,4},{2,6},{1,5},{3,7},{8,12},{10,14},{9,13},{11,15},{16,20},{18,... | collective-permute-start | bytes 1966088 | tf_op jit(solution)/shard_map/cond/branch_1_fun/ppermute | solution.py:423
  119.3 50.4 %collective-permute-start.6 = (bf16[4,64,128]{2,1,0:T(8,128)(2,1)}, bf16[4,64,128]{2,1,0:T(8,128)(2,1)S(1)}, u32[]{:S(2)}, u32[]{:S(2)}) collective-permute-start(bf16[4,64,128]{2,1,0:T(8,128)(2,1)} %get-tuple-element.84), channel_id=1, source_target_pairs={{6,0},{7,1},{14,8},{15,9},{22,16},{23,17},{30,24},{31,25}} | collective-permute-start | bytes 196616 | tf_op jit(solution)/shard_map/cond/branch_1_fun/ppermute | solution.py:423
  169.7 2.1 copy-start.15
  169.7 3.7 %collective-permute-start.11 = (bf16[4,64,128]{2,1,0:T(8,128)(2,1)}, bf16[4,64,128]{2,1,0:T(8,128)(2,1)}, u32[]{:S(2)}, u32[]{:S(2)}) collective-permute-start(bf16[4,64,128]{2,1,0:T(8,128)(2,1)} %get-tuple-element.89), channel_id=1, source_target_pairs={{0,6},{1,7},{8,14},{9,15},{16,22},{17,23},{24,30},{25,31}} | collective-permute-start | bytes 196616 | tf_op jit(solution)/shard_map/cond/branch_1_fun/ppermute | solution.py:423
  173.4 9.8 %copy-start.2 = (bf16[8,8,128,128]{3,2,1,0:T(8,128)(2,1)}, bf16[8,8,128,128]{3,2,1,0:T(8,128)(2,1)S(1)}, u32[]{:S(2)}) copy-start(bf16[8,8,128,128]{3,2,1,0:T(8,128)(2,1)S(1)} %all-to-all-done.3) | copy-start | bytes 6291460 | tf_op jit(solution)/shard_map/cond
  276.7 1.3 copy-start.4
